TPU v7x, 256 devices: a whole 4x4x8 slice. The times are simulated.
256 devices in a mesh: gx: 4 (over x), gy: 4 (over y_lo, core), gz: 16 (over z, y_hi).
Axes of the slice: x: 4, y: 4 (y_hi: 2, y_lo: 2; y = y_hi * 2 + y_lo), z: 8, core: 2. Of those that a mesh axis runs over, the one named last changes fastest.
Arguments:
- left_modes: bfloat16 [2, 4, 2, 128, 3, 131072], P(None, None, None, None, None, ('gx', 'gy', 'gz')), may hold values from -0.14160156 to 0.14160156
- right_modes: bfloat16 [2, 4, 2, 128, 3, 131072], P(None, None, None, None, None, ('gx', 'gy', 'gz')), may hold values from -0.14160156 to 0.14160156
- gamma_cols: int32 [16, 4], replicated, may hold values from 0 to 3, each once within a row
- gamma_phase: int32 [16, 4], replicated, may hold values from 0 to 3
- dilution: int32 [64], replicated, may hold values from 0 to 3
- time_pairs: int32 [4, 2], replicated, may hold values from 0 to 1
Outputs:
- meson_fields: float32 [16, 2, 2, 128, 128], P('gz', None, None, ('gx', 'gy'))
- traces: float32 [4, 16, 16, 2], P(None, 'gz')
Inputs may be any that keep to these rules, and one draw needn't show every extreme that they name: Each row of gamma_cols is a permutation of the four spins.
All inputs are finite; a program needn't handle non-finite values.
Results may differ from a plain program's by a relative error of at most 0.0003.
Values sent between devices are 32-bit elements; how exact they have to be, the bound alone decides.
No kernel may reach another device: no remote copies, remote signals or barrier semaphores. Data moves between devices by JAX's collectives and lax.ppermute only.
A program may use at most 128 MiB of HBM per device.

v0:
```python
import jax
import jax.numpy as jnp
from jax import lax
from jax.sharding import PartitionSpec as P

EXACT = lax.Precision.HIGHEST


def coefficients(gamma_cols, gamma_phase):
    spin_ids = jnp.arange(4, dtype=jnp.int32)
    onehot = (gamma_cols[:, :, None] == spin_ids[None, None, :]).astype(jnp.float32)
    real_sign = (gamma_phase == 0).astype(jnp.float32) - (gamma_phase == 2).astype(jnp.float32)
    imag_sign = (gamma_phase == 1).astype(jnp.float32) - (gamma_phase == 3).astype(jnp.float32)
    return (onehot * real_sign[:, :, None], onehot * imag_sign[:, :, None])


def select_pairs(crossed, time_pairs):
    time_ids = jnp.arange(crossed.shape[1], dtype=jnp.int32)
    first_time = (time_pairs[:, 0:1] == time_ids[None, :]).astype(jnp.float32)
    second_time = (time_pairs[:, 1:2] == time_ids[None, :]).astype(jnp.float32)
    chosen = jnp.einsum("pt,pu,gtahub->pgahb", first_time, second_time, crossed, precision=EXACT)
    real_part = chosen[:, :, 0, :, 0] - chosen[:, :, 1, :, 1]
    imag_part = chosen[:, :, 0, :, 1] + chosen[:, :, 1, :, 0]
    return jnp.stack([real_part, imag_part], axis=-1)


def project(coef_re, coef_im, pair_re, pair_im, form, part_axis):
    meson_re = jnp.einsum(form, coef_re, pair_re, precision=EXACT) - jnp.einsum(
        form, coef_im, pair_im, precision=EXACT
    )
    meson_im = jnp.einsum(form, coef_re, pair_im, precision=EXACT) + jnp.einsum(
        form, coef_im, pair_re, precision=EXACT
    )
    return jnp.stack([meson_re, meson_im], axis=part_axis)


def finish_whole(summed, time_pairs, local_gammas, block_rows, mode_count):
    group_start = lax.axis_index("gz") * local_gammas
    my_gammas = lax.dynamic_slice_in_dim(summed, group_start, local_gammas, 0)
    row_block = lax.axis_index("gx") * lax.axis_size("gy") + lax.axis_index("gy")
    meson_fields = lax.dynamic_slice_in_dim(my_gammas, row_block * block_rows, block_rows, 3)
    crossed = jnp.einsum("gtaij,hubji->gtahub", my_gammas, summed, precision=EXACT)
    traces = select_pairs(crossed, time_pairs) / mode_count
    return (meson_fields, traces)


def local(left_modes, right_modes, gamma_cols, gamma_phase, dilution, time_pairs):
    times_held = left_modes.shape[0]
    mode_count = left_modes.shape[3]
    gamma_count = gamma_cols.shape[0]
    noise_count = dilution.shape[0]
    low_count = mode_count - noise_count
    coef_re, coef_im = coefficients(gamma_cols, gamma_phase)
    groups = lax.axis_size("gz")
    blocks = lax.axis_size("gx") * lax.axis_size("gy")
    local_gammas = gamma_count // groups
    block_rows = mode_count // blocks
    spin_ids = jnp.arange(4, dtype=jnp.int32)
    noise_onehot = dilution[None, :] == spin_ids[:, None]
    select_table = noise_onehot.astype(jnp.bfloat16)
    low_re_list = []
    low_im_list = []
    noise_re_list = []
    noise_im_list = []
    for time_slot in range(times_held):
        left_slot = left_modes[time_slot]
        right_slot = right_modes[time_slot]
        low_prod = jnp.einsum(
            "spicx,qrjcx->sqpirj",
            left_slot,
            right_slot[:, :, :low_count],
            preferred_element_type=jnp.float32,
        )
        noise_right = jnp.sum(
            right_slot[:, :, low_count:] * select_table[:, None, :, None, None], axis=0
        )
        noise_prod = jnp.einsum(
            "spicx,qjcx->spiqj", left_slot, noise_right, preferred_element_type=jnp.float32
        )
        low_re_list.append(low_prod[:, :, 0, :, 0, :] + low_prod[:, :, 1, :, 1, :])
        low_im_list.append(low_prod[:, :, 0, :, 1, :] - low_prod[:, :, 1, :, 0, :])
        noise_re_list.append(noise_prod[:, 0, :, 0, :] + noise_prod[:, 1, :, 1, :])
        noise_im_list.append(noise_prod[:, 0, :, 1, :] - noise_prod[:, 1, :, 0, :])
    low_re, low_im, noise_re, noise_im = lax.psum(
        (
            jnp.stack(low_re_list),
            jnp.stack(low_im_list),
            jnp.stack(noise_re_list),
            jnp.stack(noise_im_list),
        ),
        ("gx", "gy", "gz"),
    )
    noise_float = noise_onehot.astype(jnp.float32)
    noise_coef_re = jnp.einsum("gsr,rj->gsj", coef_re, noise_float, precision=EXACT)
    noise_coef_im = jnp.einsum("gsr,rj->gsj", coef_im, noise_float, precision=EXACT)
    low_part = project(coef_re, coef_im, low_re, low_im, "gsr,tsrij->gtij", 2)
    noise_part = project(noise_coef_re, noise_coef_im, noise_re, noise_im, "gsj,tsij->gtij", 2)
    summed = jnp.concatenate([low_part, noise_part], axis=4)
    meson_fields, traces = finish_whole(summed, time_pairs, local_gammas, block_rows, mode_count)
    return (meson_fields, traces)


def solution(mesh):
    return jax.shard_map(
        local,
        mesh=mesh,
        in_specs=(
            P(None, None, None, None, None, ("gx", "gy", "gz")),
            P(None, None, None, None, None, ("gx", "gy", "gz")),
            P(),
            P(),
            P(),
            P(),
        ),
        out_specs=(P("gz", None, None, ("gx", "gy"), None), P(None, "gz", None, None)),
        check_vma=False,
    )
```

profile of v0, /device:TPU:2, one launch (start us, length us, event | category | flops | bytes accessed | tf_op | source)
XLA Modules:
  0.0 340.3 jit_solution(10529417758410979270)
XLA Ops:
  7.2 3.5 %slice_bitcast_fusion = (bf16[4,2,128,3,512]{4,2,3,1,0:T(8,128)(2,1)S(1)}, bf16[4,2,128,3,512]{4,2,3,1,0:T(8,128)(2,1)S(1)}) fusion(bf16[2,4,2,128,3,512]{5,3,4,2,1,0:T(8,128)(2,1)} %param.7), kind=kLoop, calls=%fused_computation.11 | loop fusion | bytes 12582912 | tf_op jit(solution)/shard_map/squeeze | solution.py:67
  10.7 1.1 copy-done.3
  11.9 0.7 slice_bitcast_fusion.3
  12.6 0.9 fusion.19
  13.5 1.1 fusion.30
  14.7 1.8 fusion.15
  16.7 1.1 fusion.27
  17.8 1.8 fusion.12
  19.8 0.8 pad_maximum_fusion.2
  20.6 1.5 pad_maximum_fusion
  22.9 268.4 %all-reduce.3.cloned.1.call-done = (f32[2,4,128,64]{2,3,1,0:T(8,128)}, f32[2,4,128,64]{2,3,1,0:T(8,128)}, f32[2,4,4,128,64]{3,4,1,2,0:T(8,128)}, f32[2,4,4,128,64]{3,4,1,2,0:T(8,128)}) async-done(((f32[2,4,128,64]{2,3,1,0:T(8,128)}, f32[2,4,128,64]{2,3,1,0:T(8,128)}, f32[2,4,4,128,64]{3,4,1,2,0:T(8,128)}, f32[2,4,4,128,64]{3,4,1,2,0:T(8,128)}), (f32[2,4,128,64]{2,3,1,0:T(8,128)}, ...) | async-done | bytes 2621456 | tf_op jit(solution)/shard_map/psum | solution.py:84
  291.3 3.3 convolution_bitcast_fusion.2
  294.6 3.3 convolution_bitcast_fusion
  298.0 2.0 fusion.24
  300.0 2.2 fusion.26
  302.2 1.2 fusion.48
  303.4 1.2 fusion.44
  304.5 1.2 fusion.22
  305.7 1.2 fusion.21
  306.9 2.7 fusion.101
  309.6 2.0 copy-done
  311.9 17.7 %fusion = f32[2,2,16,2,2,1]{2,1,5,4,3,0:T(2,128)S(1)} fusion(f32[2,2,128,128,1,1]{3,1,2,5,4,0:T(2,128)S(1)} %copy.67, f32[16,2,2,128,128,1]{3,0,4,1,2,5:T(8,128)} %get-tuple-element.14), kind=kOutput, calls=%fused_computation.1 | convolution fusion | flops 50331648 | bytes 4457472 | tf_op jit(solution)/shard_map/gtaij,hubji->gtahub/dot_general | solution.py:42
  330.5 2.2 constant_dynamic-slice_fusion.1
  332.7 0.7 copy.34
  (40 shorter events, 2.2 us)
Async XLA Ops:
  7.2 3.6 %copy-start.7 = (s32[64]{0:T(128)S(1)}, s32[64]{0:T(128)}, u32[]{:S(2)}) copy-start(s32[64]{0:T(128)} %param.10) | copy-start | bytes 772
  7.2 284.1 %all-reduce.3.cloned.1.call-start = ((), (), s32[]{:S(2)}) async-start(), calls=%async_computation | async-start | bytes 5242880 | tf_op jit(solution)/shard_map/psum | solution.py:84
  7.2 4.6 %copy-start.3 = (bf16[2,4,2,128,3,512]{5,3,4,2,1,0:T(8,128)(2,1)S(1)}, bf16[2,4,2,128,3,512]{5,3,4,2,1,0:T(8,128)(2,1)}, u32[]{:S(2)}) copy-start(bf16[2,4,2,128,3,512]{5,3,4,2,1,0:T(8,128)(2,1)} %param.6) | copy-start | bytes 18874372
  20.6 1.5 copy-start.8
  20.6 1.6 copy-start.6
  20.6 2.3 copy-start.9
  291.3 6.6 %copy-start.2 = (f32[2,4,4,128,64]{3,4,1,2,0:T(8,128)S(1)}, f32[2,4,4,128,64]{3,4,1,2,0:T(8,128)}, u32[]{:S(2)}) copy-start(f32[2,4,4,128,64]{3,4,1,2,0:T(8,128)} %get-tuple-element.8) | copy-start | bytes 3145732
  294.6 5.4 %copy-start.1 = (f32[2,4,4,128,64]{3,4,1,2,0:T(8,128)S(1)}, f32[2,4,4,128,64]{3,4,1,2,0:T(8,128)}, u32[]{:S(2)}) copy-start(f32[2,4,4,128,64]{3,4,1,2,0:T(8,128)} %get-tuple-element.9) | copy-start | bytes 3145732
  298.0 4.2 %copy-start.4 = (f32[2,4,128,64]{2,3,1,0:T(8,128)S(1)}, f32[2,4,128,64]{2,3,1,0:T(8,128)}, u32[]{:S(2)}) copy-start(f32[2,4,128,64]{2,3,1,0:T(8,128)} %get-tuple-element.7) | copy-start | bytes 786436
  298.0 5.4 %copy-start.5 = (f32[2,4,128,64]{2,3,1,0:T(8,128)S(1)}, f32[2,4,128,64]{2,3,1,0:T(8,128)}, u32[]{:S(2)}) copy-start(f32[2,4,128,64]{2,3,1,0:T(8,128)} %get-tuple-element.6) | copy-start | bytes 786436
  309.6 2.0 copy-start
Sparse Core Ops, SparseCore 0:
  22.3 268.9 all-reduce.2
where the time goes:
time: 340 us
  waiting for transfers between devices  268 us (79%)
  matrix products  39.7 us (12%)
  between operations  14.4 us (4%)
  local copies, waits for them, and re-layouts  11.4 us (3%)
  other arithmetic  6.28 us (2%)
    psum x1, waiting for transfers between devices, local(): lax.psum((jnp.stack(low_re_list), jnp.stack(low_im_list), jnp.stack(noise...  268 us
    dot_general x1, matrix products, finish_whole(): jnp.einsum('gtaij,hubji->gtahub', my_gammas, summed, precision=EXACT)  17.7 us
  transfers between devices with their start and end apart: 1, of which 1 were waited for; matrix products, arithmetic and copies ran while one was open for 0% of the time, Pallas kernels for 0%

commit v1 on v0

--- a/solution.py
+++ b/solution.py
@@ -82,13 +82,16 @@
         noise_re_list.append(noise_prod[:, 0, :, 0, :] + noise_prod[:, 1, :, 1, :])
         noise_im_list.append(noise_prod[:, 0, :, 1, :] - noise_prod[:, 1, :, 0, :])
     low_re, low_im, noise_re, noise_im = lax.psum(
-        (
-            jnp.stack(low_re_list),
-            jnp.stack(low_im_list),
-            jnp.stack(noise_re_list),
-            jnp.stack(noise_im_list),
+        lax.psum(
+            (
+                jnp.stack(low_re_list),
+                jnp.stack(low_im_list),
+                jnp.stack(noise_re_list),
+                jnp.stack(noise_im_list),
+            ),
+            axis_name="gx",
         ),
-        ("gx", "gy", "gz"),
+        axis_name=("gy", "gz"),
     )
     noise_float = noise_onehot.astype(jnp.float32)
     noise_coef_re = jnp.einsum("gsr,rj->gsj", coef_re, noise_float, precision=EXACT)

time: 340 us -> 343 us (level)
    psum x0 -> x1, waiting for transfers between devices: none -> 197 us  [local(): lax.psum(lax.psum((jnp.stack(low_re_list), jnp.stack(low_im_list), jnp.st...]
    psum x1, waiting for transfers between devices: 268 us -> 74.1 us  [local(): lax.psum((jnp.stack(low_re_list), jnp.stack(low_im_list), jnp.stack(noise...]
  transfers between devices with their start and end apart: 1 -> 2, of which waited for: 1 -> 2; matrix products, arithmetic and copies ran while one was open for 0% -> 0% of each run, Pallas kernels for 0% -> 0%
where the time goes in v1:
time: 343 us
  waiting for transfers between devices  271 us (79%)
  matrix products  39.5 us (12%)
  between operations  14.4 us (4%)
  local copies, waits for them, and re-layouts  11.4 us (3%)
  other arithmetic  6.25 us (2%)
    psum x1, waiting for transfers between devices, local(): lax.psum(lax.psum((jnp.stack(low_re_list), jnp.stack(low_im_list), jnp.st...  197 us
    psum x1, waiting for transfers between devices, local(): lax.psum((jnp.stack(low_re_list), jnp.stack(low_im_list), jnp.stack(noise...  74.1 us
    dot_general x1, matrix products, finish_whole(): jnp.einsum('gtaij,hubji->gtahub', my_gammas, summed, precision=EXACT)  17.5 us
  transfers between devices with their start and end apart: 2, of which 2 were waited for; matrix products, arithmetic and copies ran while one was open for 0% of the time, Pallas kernels for 0%

profile of v1, /device:TPU:2, one launch (start us, length us, event | category | flops | bytes accessed | tf_op | source)
XLA Modules:
  0.0 342.6 jit_solution(10523657598626705709)
XLA Ops:
  7.2 3.5 %slice_bitcast_fusion = (bf16[4,2,128,3,512]{4,2,3,1,0:T(8,128)(2,1)S(1)}, bf16[4,2,128,3,512]{4,2,3,1,0:T(8,128)(2,1)S(1)}) fusion(bf16[2,4,2,128,3,512]{5,3,4,2,1,0:T(8,128)(2,1)} %param.7), kind=kLoop, calls=%fused_computation.11 | loop fusion | bytes 12582912 | tf_op jit(solution)/shard_map/squeeze | solution.py:67
  10.7 1.1 copy-done.3
  11.9 0.7 slice_bitcast_fusion.3
  12.6 0.9 fusion.19
  13.5 1.1 fusion.30
  14.7 1.8 fusion.15
  16.7 1.1 fusion.27
  17.8 1.8 fusion.12
  19.8 0.8 pad_maximum_fusion.2
  20.6 1.5 pad_maximum_fusion
  22.4 74.1 %all-reduce.7.cloned.1.call-done = (f32[2,4,128,64]{2,3,1,0:T(8,128)}, f32[2,4,128,64]{2,3,1,0:T(8,128)}, f32[2,4,4,128,64]{3,4,1,2,0:T(8,128)}, f32[2,4,4,128,64]{3,4,1,2,0:T(8,128)}) async-done(((f32[2,4,128,64]{2,3,1,0:T(8,128)}, f32[2,4,128,64]{2,3,1,0:T(8,128)}, f32[2,4,4,128,64]{3,4,1,2,0:T(8,128)}, f32[2,4,4,128,64]{3,4,1,2,0:T(8,128)}), (f32[2,4,128,64]{2,3,1,0:T(8,128)}, ...) | async-done | bytes 2621456 | tf_op jit(solution)/shard_map/psum | solution.py:85
  97.2 196.6 %all-reduce.5.cloned.1.call-done = (f32[2,4,128,64]{2,3,1,0:T(8,128)}, f32[2,4,128,64]{2,3,1,0:T(8,128)}, f32[2,4,4,128,64]{3,4,1,2,0:T(8,128)}, f32[2,4,4,128,64]{3,4,1,2,0:T(8,128)}) async-done(((f32[2,4,128,64]{2,3,1,0:T(8,128)}, f32[2,4,128,64]{2,3,1,0:T(8,128)}, f32[2,4,4,128,64]{3,4,1,2,0:T(8,128)}, f32[2,4,4,128,64]{3,4,1,2,0:T(8,128)}), (f32[2,4,128,64]{2,3,1,0:T(8,128)}, ...) | async-done | bytes 2621456 | tf_op jit(solution)/shard_map/psum | solution.py:84
  293.8 3.3 convolution_bitcast_fusion.2
  297.2 3.3 convolution_bitcast_fusion
  300.5 2.0 fusion.24
  302.5 2.0 fusion.26
  304.5 1.2 fusion.48
  305.7 1.2 fusion.44
  306.9 1.2 fusion.22
  308.1 1.4 fusion.21
  309.5 2.7 fusion.101
  312.1 2.0 copy-done
  314.5 17.5 %fusion = f32[2,2,16,2,2,1]{2,1,5,4,3,0:T(2,128)S(1)} fusion(f32[2,2,128,128,1,1]{3,1,2,5,4,0:T(2,128)S(1)} %copy.67, f32[16,2,2,128,128,1]{3,0,4,1,2,5:T(8,128)} %get-tuple-element.18), kind=kOutput, calls=%fused_computation.1 | convolution fusion | flops 50331648 | bytes 4457472 | tf_op jit(solution)/shard_map/gtaij,hubji->gtahub/dot_general | solution.py:42
  332.8 2.2 constant_dynamic-slice_fusion.1
  (43 shorter events, 3.2 us)
Async XLA Ops:
  7.2 3.6 %copy-start.7 = (s32[64]{0:T(128)S(1)}, s32[64]{0:T(128)}, u32[]{:S(2)}) copy-start(s32[64]{0:T(128)} %param.10) | copy-start | bytes 772
  7.2 89.3 %all-reduce.7.cloned.1.call-start = ((), (), s32[]{:S(2)}) async-start(), calls=%async_computation.1 | async-start | bytes 5242880 | tf_op jit(solution)/shard_map/psum | solution.py:85
  7.2 4.6 %copy-start.3 = (bf16[2,4,2,128,3,512]{5,3,4,2,1,0:T(8,128)(2,1)S(1)}, bf16[2,4,2,128,3,512]{5,3,4,2,1,0:T(8,128)(2,1)}, u32[]{:S(2)}) copy-start(bf16[2,4,2,128,3,512]{5,3,4,2,1,0:T(8,128)(2,1)} %param.6) | copy-start | bytes 18874372
  22.1 74.3 %copy-start.8 = (s32[16,4]{0,1:T(4,128)S(1)}, s32[16,4]{0,1:T(4,128)}, u32[]{:S(2)}) copy-start(s32[16,4]{0,1:T(4,128)} %param.9) | copy-start | bytes 772
  22.1 74.4 %copy-start.6 = (s32[16,4]{0,1:T(4,128)S(1)}, s32[16,4]{0,1:T(4,128)}, u32[]{:S(2)}) copy-start(s32[16,4]{0,1:T(4,128)} %param.8) | copy-start | bytes 772
  22.1 75.1 %copy-start.9 = (s32[4,2]{0,1:T(2,128)S(1)}, s32[4,2]{0,1:T(2,128)}, u32[]{:S(2)}) copy-start(s32[4,2]{0,1:T(2,128)} %param.11) | copy-start | bytes 100
  22.2 271.7 %all-reduce.5.cloned.1.call-start = ((), (), s32[]{:S(2)}) async-start(), calls=%async_computation | async-start | bytes 5242880 | tf_op jit(solution)/shard_map/psum | solution.py:84
  293.8 6.6 %copy-start.2 = (f32[2,4,4,128,64]{3,4,1,2,0:T(8,128)S(1)}, f32[2,4,4,128,64]{3,4,1,2,0:T(8,128)}, u32[]{:S(2)}) copy-start(f32[2,4,4,128,64]{3,4,1,2,0:T(8,128)} %get-tuple-element.8) | copy-start | bytes 3145732
  297.1 5.4 %copy-start.1 = (f32[2,4,4,128,64]{3,4,1,2,0:T(8,128)S(1)}, f32[2,4,4,128,64]{3,4,1,2,0:T(8,128)}, u32[]{:S(2)}) copy-start(f32[2,4,4,128,64]{3,4,1,2,0:T(8,128)} %get-tuple-element.9) | copy-start | bytes 3145732
  300.5 4.0 %copy-start.4 = (f32[2,4,128,64]{2,3,1,0:T(8,128)S(1)}, f32[2,4,128,64]{2,3,1,0:T(8,128)}, u32[]{:S(2)}) copy-start(f32[2,4,128,64]{2,3,1,0:T(8,128)} %get-tuple-element.7) | copy-start | bytes 786436
  300.5 5.2 %copy-start.5 = (f32[2,4,128,64]{2,3,1,0:T(8,128)S(1)}, f32[2,4,128,64]{2,3,1,0:T(8,128)}, u32[]{:S(2)}) copy-start(f32[2,4,128,64]{2,3,1,0:T(8,128)} %get-tuple-element.6) | copy-start | bytes 786436
  312.1 2.0 copy-start
Sparse Core Ops, SparseCore 0:
  22.3 74.1 all-reduce.6
  100.4 193.4 all-reduce.4
